TPU v7x, 128 devices: a whole 4x4x4 slice. The times are simulated.
128 devices in a mesh: expert: 4 (over y_lo, core), shard: 32 (over z, y_hi, x).
Axes of the slice: x: 4, y: 4 (y_hi: 2, y_lo: 2; y = y_hi * 2 + y_lo), z: 4, core: 2. Of those that a mesh axis runs over, the one named last changes fastest.
Arguments:
- train_down: float32 [16, 6400, 4096], P('expert', None, 'shard'), may hold values from -0.15625 to 0.15625
- other_down: bfloat16 [16, 6400, 4096], P('expert', None, 'shard'), may hold values from -0.0390625 to 0.0390625
- router_weight: float32 [4096, 16], P('shard', 'expert'), may hold values from -0.09375 to 0.09375
- router_gain: float32 [4096], P('shard'), may hold values from 0.25 to 1.75
Outputs:
- ready_down: bfloat16 [16, 6400, 4096], P('expert', 'shard')
- scale_down: float32 [16, 6400], P('expert', 'shard')
- serve_router: bfloat16 [4096, 16], replicated
All inputs are finite; a program needn't handle non-finite values.
Results may differ from a plain program's by a relative error of at most 0.001.
Values may be sent and summed in bfloat16 or wider, within the bound.
A program may use at most 128 MiB of HBM per device.

v0:
```python
import jax
import jax.numpy as jnp
from jax import lax
from jax.sharding import PartitionSpec as P


def copy_for_each(x, axis):
    length = lax.axis_size(axis)
    return lax.all_to_all(jnp.broadcast_to(x[None], (length, *x.shape)), axis, 0, 0, tiled=True)


def of_everyone(x, axis):
    everything = copy_for_each(x, axis)
    return jnp.sum(everything, axis=0)


def in_blocks(x, dim, length):
    before, after = (x.shape[:dim], x.shape[dim + 1 :])
    return jnp.moveaxis(x.reshape(*before, length, -1, *after), dim, 0)


def piece_ends(length, count):
    unit = 8 if length >= 8 * count else 1
    return [length // unit * k // count * unit for k in range(1, count)]


def in_order(pieces, dim):
    pieces = jnp.moveaxis(pieces, 0, dim)
    dims = pieces.shape
    return pieces.reshape(*dims[:dim], dims[dim] * dims[dim + 1], *dims[dim + 2 :])


def exchange_in_pieces(x, axis, pieces, split_dim, concat_dim):
    blocks = in_blocks(x, split_dim, lax.axis_size(axis))
    split_at = max(range(1, max(2, blocks.ndim - 1)), key=lambda d: blocks.shape[d])
    gathered = []
    for slab in jnp.split(blocks, piece_ends(blocks.shape[split_at], pieces), axis=split_at):
        if slab.size:
            gathered.append(lax.all_to_all(slab, axis, split_axis=0, concat_axis=0, tiled=True))
    return in_order(jnp.concatenate(gathered, axis=split_at), concat_dim)


def gathered_copies(x, axis, dim):
    pieces = copy_for_each(x, axis)
    return in_order(pieces, dim)


def per_device(train_down, other_down, router_weight, router_gain):
    latest_down = train_down + other_down.astype(jnp.float32)
    total_down = of_everyone(jnp.sum(latest_down * latest_down, axis=2), "shard")
    scale_down = jnp.sqrt(total_down)
    narrow_down = (latest_down / jnp.expand_dims(scale_down, 2)).astype(jnp.bfloat16)
    ready_down = exchange_in_pieces(narrow_down, "shard", 2, 1, 2)
    scale_down = lax.dynamic_slice_in_dim(
        scale_down, lax.axis_index("shard") * ready_down.shape[1], ready_down.shape[1], axis=1
    )
    part_router = (router_weight * router_gain[:, None]).astype(jnp.bfloat16)
    row_router = gathered_copies(part_router, "shard", 0)
    serve_router = gathered_copies(row_router, "expert", 1)
    return (ready_down, scale_down, serve_router)


def solution(mesh):
    in_specs = (
        P("expert", None, "shard"),
        P("expert", None, "shard"),
        P("shard", "expert"),
        P("shard"),
    )
    out_specs = (P("expert", "shard", None), P("expert", "shard"), P())
    return jax.shard_map(
        per_device, mesh=mesh, in_specs=in_specs, out_specs=out_specs, check_vma=False
    )
```

profile of v0, /device:TPU:18, one launch (start us, length us, event | category | flops | bytes accessed | tf_op | source)
XLA Modules:
  0.0 207.1 jit_solution(8176549847378786025)
XLA Ops:
  0.6 0.7 multiply_convert_fusion
  1.3 0.6 broadcast_in_dim.9
  1.9 10.9 %all-to-all-start.3 = ((bf16[32,128,4]{1,2,0:T(4,128)(2,1)}), bf16[32,128,4]{1,2,0:T(4,128)(2,1)S(1)}, u32[]{:S(2)}, u32[]{:S(2)}) async-start(bf16[32,128,4]{1,2,0:T(4,128)(2,1)} %broadcast_in_dim.9), calls=%async_computation.3 | async-start | bytes 65536 | tf_op jit(solution)/shard_map/all_to_all | solution.py:9
  12.8 8.3 %multiply_reduce_fusion = f32[4,6400]{1,0:T(4,128)S(1)} fusion(f32[4,6400,128]{2,1,0:T(8,128)} %param.4, bf16[4,6400,128]{2,1,0:T(8,128)(2,1)} %param.5), kind=kLoop, calls=%fused_computation.1 | loop fusion | flops 13081600 | bytes 19763200 | tf_op jit(solution)/shard_map/reduce_sum | solution.py:50
  21.2 0.4 broadcast_in_dim.8
  21.6 48.7 %all_to_all.25 = f32[32,4,6400]{2,1,0:T(4,128)S(1)} all-to-all(f32[32,4,6400]{2,1,0:T(4,128)S(1)} %broadcast_in_dim.8), channel_id=1, replica_groups=mesh['expert'=4,'shard'=32] {'shard'}, dimensions={0} | all-to-all | bytes 6553600 | tf_op jit(solution)/shard_map/all_to_all | solution.py:9
  70.3 0.7 broadcast_in_dim.11
  71.0 3.3 %all-to-all-start.4 = ((bf16[4,4096,4]{1,2,0:T(4,128)(2,1)}), bf16[4,4096,4]{1,2,0:T(4,128)(2,1)S(1)}, u32[]{:S(2)}, u32[]{:S(2)}) async-start(bf16[4,4096,4]{1,2,0:T(4,128)(2,1)} %broadcast_in_dim.11), calls=%async_computation.4 | async-start | bytes 262144 | tf_op jit(solution)/shard_map/all_to_all | solution.py:9
  74.3 0.5 reduce_sum.19
  74.9 0.1 sqrt.7
  74.9 11.0 %divide_convert_fusion = bf16[4,6400,128]{2,1,0:T(8,128)(2,1)S(1)} fusion(f32[4,6400,128]{2,1,0:T(8,128)} %param.4, bf16[4,6400,128]{2,1,0:T(8,128)(2,1)} %param.5, f32[4,6400]{1,0:T(4,128)S(1)} %sqrt.7), kind=kLoop, calls=%fused_computation | loop fusion | flops 13107200 | bytes 26316800 | tf_op jit(solution)/shard_map/convert_element_type | solution.py:52
  86.0 2.8 %copy-done = bf16[4,6400,128]{2,1,0:T(8,128)(2,1)} copy-done((bf16[4,6400,128]{2,1,0:T(8,128)(2,1)}, bf16[4,6400,128]{2,1,0:T(8,128)(2,1)S(1)}, u32[]{:S(2)}) %copy-start) | copy-done | bytes 6553624
  88.8 0.3 split.8
  89.1 2.1 %copy.15 = bf16[32,4,96,128]{3,2,1,0:T(8,128)(2,1)} copy(bf16[32,4,96,128]{3,2,0,1:T(8,128)(2,1)S(1)} %split.8) | data formatting | bytes 6291456 | tf_op jit(solution)/shard_map/split | solution.py:37
  91.2 7.5 %all-to-all-start.1 = ((bf16[32,4,96,128]{3,2,1,0:T(8,128)(2,1)}), bf16[32,4,96,128]{3,2,1,0:T(8,128)(2,1)S(1)}, u32[]{:S(2)}, u32[]{:S(2)}) async-start(bf16[32,4,96,128]{3,2,1,0:T(8,128)(2,1)} %copy.15), calls=%async_computation.1 | async-start | bytes 6291456 | tf_op jit(solution)/shard_map/all_to_all | solution.py:39
  98.7 2.2 %split.9 = bf16[32,4,104,128]{3,2,0,1:T(8,128)(2,1)S(1)} slice(bf16[32,4,200,128]{3,2,0,1:T(8,128)(2,1)} %bitcast.14), slice={[0:32], [0:4], [96:200], [0:128]} | slice | bytes 6815744 | tf_op jit(solution)/shard_map/split | solution.py:37
  101.0 2.0 copy.16
  103.0 42.9 %all-to-all-done.1 = bf16[32,4,96,128]{3,2,1,0:T(8,128)(2,1)S(1)} async-done(((bf16[32,4,96,128]{3,2,1,0:T(8,128)(2,1)}), bf16[32,4,96,128]{3,2,1,0:T(8,128)(2,1)S(1)}, u32[]{:S(2)}, u32[]{:S(2)}) %all-to-all-start.1) | async-done | bytes 3145760 | tf_op jit(solution)/shard_map/all_to_all | solution.py:39
  145.9 1.7 copy-done.1
  147.5 5.9 %all-to-all-start.2 = ((bf16[32,4,104,128]{3,2,1,0:T(8,128)(2,1)}), bf16[32,4,104,128]{3,2,1,0:T(8,128)(2,1)S(1)}, u32[]{:S(2)}, u32[]{:S(2)}) async-start(bf16[32,4,104,128]{3,2,1,0:T(8,128)(2,1)} %copy.16), calls=%async_computation.2 | async-start | bytes 6815744 | tf_op jit(solution)/shard_map/all_to_all | solution.py:39
  153.4 0.7 reshape.24
  154.1 1.4 constant_dynamic-slice_fusion
  155.5 46.0 %all-to-all-done.2 = bf16[32,4,104,128]{3,2,1,0:T(8,128)(2,1)S(1)} async-done(((bf16[32,4,104,128]{3,2,1,0:T(8,128)(2,1)}), bf16[32,4,104,128]{3,2,1,0:T(8,128)(2,1)S(1)}, u32[]{:S(2)}, u32[]{:S(2)}) %all-to-all-start.2) | async-done | bytes 3407904 | tf_op jit(solution)/shard_map/all_to_all | solution.py:39
  201.5 5.6 %copy_bitcast_fusion = bf16[4,200,4096]{2,1,0:T(8,128)(2,1)} fusion(bf16[32,4,104,128]{3,2,1,0:T(8,128)(2,1)S(1)} %all-to-all-done.2, bf16[32,4,96,128]{3,2,1,0:T(8,128)(2,1)} %copy-done.1), kind=kLoop, calls=%fused_computation.3 | loop fusion | flops 13107200 | bytes 13107200 | tf_op jit(solution)/shard_map/reshape | solution.py:30
  (6 shorter events, 0.0 us)
Async XLA Ops:
  1.9 19.2 %all-to-all-start.3 = ((bf16[32,128,4]{1,2,0:T(4,128)(2,1)}), bf16[32,128,4]{1,2,0:T(4,128)(2,1)S(1)}, u32[]{:S(2)}, u32[]{:S(2)}) async-start(bf16[32,128,4]{1,2,0:T(4,128)(2,1)} %broadcast_in_dim.9), calls=%async_computation.3 | async-start | bytes 65536 | tf_op jit(solution)/shard_map/all_to_all | solution.py:9
  71.0 20.2 %all-to-all-start.4 = ((bf16[4,4096,4]{1,2,0:T(4,128)(2,1)}), bf16[4,4096,4]{1,2,0:T(4,128)(2,1)S(1)}, u32[]{:S(2)}, u32[]{:S(2)}) async-start(bf16[4,4096,4]{1,2,0:T(4,128)(2,1)} %broadcast_in_dim.11), calls=%async_computation.4 | async-start | bytes 262144 | tf_op jit(solution)/shard_map/all_to_all | solution.py:9
  74.9 11.0 %copy-start.2 = (f32[4,6400]{1,0:T(4,128)}, f32[4,6400]{1,0:T(4,128)S(1)}, u32[]{:S(2)}) copy-start(f32[4,6400]{1,0:T(4,128)S(1)} %sqrt.7) | copy-start | bytes 307204
  86.0 2.8 %copy-start = (bf16[4,6400,128]{2,1,0:T(8,128)(2,1)}, bf16[4,6400,128]{2,1,0:T(8,128)(2,1)S(1)}, u32[]{:S(2)}) copy-start(bf16[4,6400,128]{2,1,0:T(8,128)(2,1)S(1)} %divide_convert_fusion) | copy-start | bytes 19660804
  91.2 54.7 %all-to-all-start.1 = ((bf16[32,4,96,128]{3,2,1,0:T(8,128)(2,1)}), bf16[32,4,96,128]{3,2,1,0:T(8,128)(2,1)S(1)}, u32[]{:S(2)}, u32[]{:S(2)}) async-start(bf16[32,4,96,128]{3,2,1,0:T(8,128)(2,1)} %copy.15), calls=%async_computation.1 | async-start | bytes 6291456 | tf_op jit(solution)/shard_map/all_to_all | solution.py:39
  145.9 1.7 copy-start.1
  147.5 53.9 %all-to-all-start.2 = ((bf16[32,4,104,128]{3,2,1,0:T(8,128)(2,1)}), bf16[32,4,104,128]{3,2,1,0:T(8,128)(2,1)S(1)}, u32[]{:S(2)}, u32[]{:S(2)}) async-start(bf16[32,4,104,128]{3,2,1,0:T(8,128)(2,1)} %copy.16), calls=%async_computation.2 | async-start | bytes 6815744 | tf_op jit(solution)/shard_map/all_to_all | solution.py:39
where the time goes:
time: 208 us; the launch traced here: 207 us
  waiting for transfers between devices  88.9 us (43%)
  blocking collectives  48.7 us (23%)
  starting transfers between devices  27.6 us (13%)
  other arithmetic  26.2 us (13%)
  local copies, waits for them, and re-layouts  14.9 us (7%)
    all_to_all x2, waiting for transfers between devices, exchange_in_pieces(): lax.all_to_all(slab, axis, split_axis=0, concat_axis=0, tiled=True)  88.9 us
    all_to_all x1, blocking collectives, copy_for_each(): lax.all_to_all(jnp.broadcast_to(x[None], (length, *x.shape)), axis, 0, 0,...  48.7 us
    all_to_all x2, starting transfers between devices, copy_for_each(): lax.all_to_all(jnp.broadcast_to(x[None], (length, *x.shape)), axis, 0, 0,...  14.2 us
    all_to_all x2, starting transfers between devices, exchange_in_pieces(): lax.all_to_all(slab, axis, split_axis=0, concat_axis=0, tiled=True)  13.4 us
    convert_element_type x1, other arithmetic, per_device(): (latest_down / jnp.expand_dims(scale_down, 2)).astype(jnp.bfloat16)  11 us
    reduce_sum x1, other arithmetic, per_device(): jnp.sum(latest_down * latest_down, axis=2)  8.33 us
    split x4, local copies, waits for them, and re-layouts, exchange_in_pieces(): jnp.split(blocks, piece_ends(blocks.shape[split_at], pieces), axis=split_at)  6.63 us
    reshape x1, other arithmetic, in_order(): pieces.reshape(*dims[:dim], dims[dim] * dims[dim + 1], *dims[dim + 2:])  5.64 us
  transfers between devices with their start and end apart: 4, of which 2 were waited for; matrix products, arithmetic and copies ran while one was open for 14% of the time, Pallas kernels for 0%

commit v1 on v0

v1 whole, which is shorter than its diff:
```python
import functools

import jax
import jax.numpy as jnp
from jax import lax
from jax.experimental import pallas as pl
from jax.experimental.pallas import tpu as pltpu
from jax.sharding import PartitionSpec as P

MESH = pl.DeviceIdType.MESH
F32 = jnp.float32
BF16 = jnp.bfloat16
SPAN = 240.0
HALF = 120.0
LN2 = 0.6931471805599453
TINY = 1e-37


def coords(shard):
    return shard // 8, (shard // 4) % 2, shard % 4


def ahead(me, off):
    z, y, x = coords(me)
    dz, dy, dx = coords(off)
    return ((z + dz) % 4) * 8 + ((y + dy) % 2) * 4 + (x + dx) % 4


def behind(me, off):
    z, y, x = coords(me)
    dz, dy, dx = coords(off)
    return ((z + 4 - dz) % 4) * 8 + ((y + 2 - dy) % 2) * 4 + (x + 4 - dx) % 4


def turn(i, e):
    return (27 * i + 9 * e) % 32


def to_all_lanes(tile, lane):
    return jnp.broadcast_to(tile[:, lane : lane + 1], tile.shape)


def exchange(train, other, weight, gain, ready, scale, router,
             tbuf, obuf, sbuf, rbuf, ssum, rsum, fbuf, part, pair, rows_in, rows_out,
             load_t, load_o, send, recv, self_sem, sum_send, sum_recv,
             pair_send, pair_recv, row_send, row_recv, core_send, core_recv):
    experts, tiles = ready.shape[0], ready.shape[1]
    me = lax.axis_index("shard")
    group = lax.axis_index("expert")
    y_lo, core = group // 2, group % 2
    across = (1 - y_lo) * 2 + core
    beside = y_lo * 2 + (1 - core)

    loads = []
    for e in range(experts):
        pair_of = (
            pltpu.make_async_copy(train.at[e], tbuf.at[e], load_t.at[e]),
            pltpu.make_async_copy(other.at[e], obuf.at[e], load_o.at[e]),
        )
        for copy in pair_of:
            copy.start()
        loads.append(pair_of)

    barrier = pltpu.get_barrier_semaphore()

    def greet(off, _):
        pl.semaphore_signal(barrier, inc=1, device_id={"shard": ahead(me, off)}, device_id_type=MESH)
        return 0

    lax.fori_loop(1, 32, greet, 0)
    for peer in (across, beside):
        pl.semaphore_signal(barrier, inc=1, device_id={"expert": peer}, device_id_type=MESH)

    lanes = lax.broadcasted_iota(jnp.int32, (8, 128), 1)

    def latest(e, j, t):
        at = j * tiles + t
        return tbuf[e, at] + obuf[e, at].astype(F32)

    def sums_of(e):
        def body(off, _):
            j = ahead(me, off)
            tile = jnp.zeros((8, 128), F32) if e == 0 else ssum[off]
            for t in range(tiles):
                x = latest(e, j, t)
                total = jnp.sum(x * x, axis=1, keepdims=True)
                tile = jnp.where(lanes == e * tiles + t, total, tile)
            ssum[off] = tile
            return 0

        for copy in loads[e]:
            copy.wait()
        lax.fori_loop(0, 32, body, 0)

    def send_piece(e, off):
        p = e * 32 + off

        @pl.when(off != 0)
        def _():
            pltpu.make_async_remote_copy(
                sbuf.at[p], rbuf.at[p], send, recv.at[p],
                device_id={"shard": ahead(me, off)}, device_id_type=MESH,
            ).start()

    def encode(e):
        def body(i, _):
            off = turn(i, e)
            p = e * 32 + off
            j = ahead(me, off)
            inverse = lax.rsqrt(jnp.maximum(ssum[off], TINY))
            for t in range(tiles):
                x = latest(e, j, t)
                share = jnp.maximum(jnp.abs(x) * to_all_lanes(inverse, e * tiles + t), 1e-30)
                root = share * lax.rsqrt(share)
                code = jnp.exp2(root * SPAN - HALF)
                sbuf[p, t] = jnp.where(x < 0, -code, code).astype(BF16)

            @pl.when(i > 0)
            def _():
                send_piece(e, turn(i + 31, e))

            return 0

        lax.fori_loop(0, 32, body, 0)
        send_piece(e, turn(31, e))

    own = weight[...] * gain[...]
    part[...] = jnp.concatenate([own, jnp.zeros_like(own)], axis=0).astype(BF16)

    sums_of(0)
    pl.semaphore_wait(barrier, 33)
    to_pair = pltpu.make_async_remote_copy(
        part, pair, pair_send, pair_recv, device_id={"expert": across}, device_id_type=MESH
    )
    to_pair.start()
    encode(0)
    for e in range(1, experts):
        sums_of(e)

    to_pair.wait()
    mine, theirs = part[...].astype(F32)[:4], pair[...].astype(F32)[:4]
    low = jnp.where(y_lo == 0, mine, theirs)
    high = jnp.where(y_lo == 0, theirs, mine)
    rows_in[0] = jnp.concatenate([low, high], axis=0).astype(BF16)
    rsum[0] = ssum[0]

    def send_small(i, _):
        off = turn(i, 0)

        @pl.when(off != 0)
        def _():
            pltpu.make_async_remote_copy(
                ssum.at[off], rsum.at[off], sum_send, sum_recv,
                device_id={"shard": ahead(me, off)}, device_id_type=MESH,
            ).start()
            pltpu.make_async_remote_copy(
                rows_in.at[0], rows_in.at[off], row_send, row_recv,
                device_id={"shard": ahead(me, off)}, device_id_type=MESH,
            ).start()

        return 0

    lax.fori_loop(0, 32, send_small, 0)
    for e in range(1, experts):
        encode(e)
    keep = [
        pltpu.make_async_copy(sbuf.at[e * 32], rbuf.at[e * 32], self_sem.at[e])
        for e in range(experts)
    ]
    for copy in keep:
        copy.start()

    rest = pltpu.make_async_remote_copy(
        ssum.at[pl.ds(1, 31)], rsum.at[pl.ds(1, 31)], sum_send, sum_recv,
        device_id={"shard": ahead(me, 1)}, device_id_type=MESH,
    )
    rest.wait_recv()
    total = lax.fori_loop(1, 32, lambda k, acc: acc + rsum[k], rsum[0])

    def factors(k, _):
        fbuf[k] = jnp.sqrt(rsum[k] / total)
        return 0

    lax.fori_loop(0, 32, factors, 0)
    norm = jnp.sqrt(total)
    wide = lax.broadcasted_iota(jnp.int32, (8, 256), 1) - lax.broadcasted_iota(jnp.int32, (8, 256), 0)
    for e in range(experts):
        spread = jnp.zeros((8, 256), F32)
        for t in range(tiles):
            column = norm[:, e * tiles + t : e * tiles + t + 1]
            spread = jnp.where(wide == t * 8, column, spread)
        scale[e : e + 1, :] = jnp.sum(spread, axis=0, keepdims=True)[:, : tiles * 8]

    def decode(e):
        def body(i, _):
            off = turn(i, e)
            p = e * 32 + off
            source = behind(me, off)

            @pl.when(off != 0)
            def _():
                pltpu.make_async_remote_copy(
                    sbuf.at[p], rbuf.at[p], send, recv.at[p],
                    device_id={"shard": source}, device_id_type=MESH,
                ).wait_recv()

            factor = fbuf[off]
            for t in range(tiles):
                y = rbuf[p, t].astype(F32)
                root = jnp.log(jnp.abs(y)) * (1.0 / (SPAN * LN2)) + HALF / SPAN
                value = root * root * to_all_lanes(factor, e * tiles + t)
                ready[e, t, source] = jnp.where(y < 0, -value, value).astype(BF16)
            return 0

        keep[e].wait()
        lax.fori_loop(0, 32, body, 0)

    decode(0)
    rows = pltpu.make_async_remote_copy(
        rows_in.at[pl.ds(1, 31)], rows_in.at[pl.ds(1, 31)], row_send, row_recv,
        device_id={"shard": ahead(me, 1)}, device_id_type=MESH,
    )
    rows.wait_recv()
    to_core = pltpu.make_async_remote_copy(
        rows_in, rows_out, core_send, core_recv, device_id={"expert": beside}, device_id_type=MESH
    )
    to_core.start()
    decode(1)
    to_core.wait()

    def place(k, _):
        a, b = rows_in[k].astype(F32), rows_out[k].astype(F32)
        first = jnp.where(core == 0, a, b)
        second = jnp.where(core == 0, b, a)
        block = jnp.concatenate([first[:4], second[:4], first[4:], second[4:]], axis=0)
        router[:, pl.ds(pl.multiple_of(behind(me, k) * 128, 128), 128)] = block.astype(BF16)
        return 0

    lax.fori_loop(0, 32, place, 0)
    for e in range(2, experts):
        decode(e)

    rest.wait_send()
    pltpu.make_async_remote_copy(
        rows_in.at[pl.ds(1, 31)], rows_in.at[pl.ds(1, 31)], row_send, row_recv,
        device_id={"shard": ahead(me, 1)}, device_id_type=MESH,
    ).wait_send()
    pltpu.make_async_remote_copy(
        sbuf.at[pl.ds(0, 31 * experts)], rbuf.at[pl.ds(0, 31 * experts)], send, recv.at[0],
        device_id={"shard": ahead(me, 1)}, device_id_type=MESH,
    ).wait_send()


def deliver(ready_in, scale_in, router_in, ready, scale, router, sems):
    copies = [
        pltpu.make_async_copy(ready_in.at[e], ready.at[e], sems.at[e]) for e in range(ready.shape[0])
    ]
    for copy in copies:
        copy.start()
    scale[...] = scale_in[...]
    router[...] = router_in[...]
    for copy in copies:
        copy.wait()


def per_device(train_down, other_down, router_weight, router_gain):
    experts, inner, columns = train_down.shape
    tiles = inner // 32 // 8
    rows = inner // 8
    train = train_down.reshape(experts, rows, 8, columns)
    other = other_down.reshape(experts, rows, 8, columns)
    vmem = pl.BlockSpec(memory_space=pltpu.VMEM)
    anywhere = pl.BlockSpec(memory_space=pl.ANY)
    dma = pltpu.SemaphoreType.DMA
    pieces = experts * 32
    inside = pl.pallas_call(
        exchange,
        out_shape=(
            pltpu.VMEM((experts, tiles, 32, 8, columns), BF16),
            pltpu.VMEM((experts, tiles * 8), F32),
            pltpu.VMEM((16, 4096), BF16),
        ),
        in_specs=[anywhere, anywhere, vmem, vmem],
        out_specs=(vmem, vmem, vmem),
        scratch_shapes=[
            pltpu.VMEM((experts, rows, 8, columns), F32),
            pltpu.VMEM((experts, rows, 8, columns), BF16),
            pltpu.VMEM((pieces, tiles, 8, columns), BF16),
            pltpu.VMEM((pieces, tiles, 8, columns), BF16),
            pltpu.VMEM((32, 8, 128), F32),
            pltpu.VMEM((32, 8, 128), F32),
            pltpu.VMEM((32, 8, 128), F32),
            pltpu.VMEM((8, 128), BF16),
            pltpu.VMEM((8, 128), BF16),
            pltpu.VMEM((32, 8, 128), BF16),
            pltpu.VMEM((32, 8, 128), BF16),
            dma((experts,)), dma((experts,)), dma, dma((pieces,)), dma((experts,)),
            dma, dma, dma, dma, dma, dma, dma, dma,
        ],
        compiler_params=pltpu.CompilerParams(
            collective_id=0, has_side_effects=True, vmem_limit_bytes=48 * 1024 * 1024
        ),
        name="exchange",
    )(train, other, router_weight.T, router_gain.reshape(1, -1))
    ready, scale, router = pl.pallas_call(
        deliver,
        out_shape=(
            jax.ShapeDtypeStruct((experts, tiles, 32, 8, columns), BF16),
            jax.ShapeDtypeStruct((experts, tiles * 8), F32),
            jax.ShapeDtypeStruct((16, 4096), BF16),
        ),
        in_specs=[vmem, vmem, vmem],
        out_specs=(anywhere, vmem, vmem),
        scratch_shapes=[dma((experts,))],
        compiler_params=pltpu.CompilerParams(vmem_limit_bytes=16 * 1024 * 1024),
        name="deliver",
    )(*inside)
    ready = ready.transpose(0, 1, 3, 2, 4).reshape(experts, tiles * 8, 32 * columns)
    return (ready, scale, router.T)


def solution(mesh):
    in_specs = (
        P("expert", None, "shard"),
        P("expert", None, "shard"),
        P("shard", "expert"),
        P("shard"),
    )
    out_specs = (P("expert", "shard", None), P("expert", "shard"), P())
    return jax.shard_map(
        per_device, mesh=mesh, in_specs=in_specs, out_specs=out_specs, check_vma=False
    )
```

time: 208 us -> 95.8 us (0.46)
  the two profiles are of different devices: /device:TPU:18 before, /device:TPU:22 now
where the time goes in v1:
time: 95.8 us; the launch traced here: 95.7 us
  Pallas kernels  95.1 us (99%)
    pallas_call x1, Pallas kernels, per_device(): pl.pallas_call(exchange, out_shape=(pltpu.VMEM((experts, tiles, 32, 8, co...  91.6 us
    pallas_call x1, Pallas kernels, per_device(): pl.pallas_call(deliver, out_shape=(jax.ShapeDtypeStruct((experts, tiles,...  3.48 us

profile of v1, /device:TPU:22, one launch (start us, length us, event | category | flops | bytes accessed | tf_op | source)
XLA Modules:
  0.0 95.7 jit_solution(11197421257872156614)
XLA Ops:
  0.6 91.6 %exchange.1 = (bf16[4,25,32,8,128]{4,3,2,1,0:T(8,128)(2,1)S(1)}, f32[4,200]{1,0:T(4,128)S(1)}, bf16[16,4096]{1,0:T(8,128)(2,1)S(1)}) custom-call(f32[4,800,8,128]{3,2,1,0:T(8,128)} %bitcast.8, bf16[4,800,8,128]{3,2,1,0:T(8,128)(2,1)} %bitcast.9, f32[4,128]{1,0:T(4,128)} %bitcast.10, f32[1,128]{1,0:T(1,128)} %bitcast.11), custom_call_target="tpu_custom_call" | custom-call | tf_op jit(solution)/shard_map/exchange/pallas_call | solution.py:276
  92.2 3.5 %deliver.1 = (bf16[4,25,32,8,128]{4,3,2,1,0:T(8,128)(2,1)}, f32[4,200]{1,0:T(4,128)}, bf16[16,4096]{1,0:T(8,128)(2,1)}) custom-call(bf16[4,25,32,8,128]{4,3,2,1,0:T(8,128)(2,1)S(1)} %get-tuple-element.9.ready_in, f32[4,200]{1,0:T(4,128)S(1)} %get-tuple-element.10.scale_in, bf16[16,4096]{1,0:T(8,128)(2,1)S(1)} %get-tuple-element.11.router_in), custom_call_target="tpu_custom_call" | custom-call | tf_op jit(solution)/shard_map/deliver/pallas_call | solution.py:305

commit v2 on v1

v2 whole, which is shorter than its diff:
```python
import functools

import jax
import jax.numpy as jnp
from jax import lax
from jax.experimental import pallas as pl
from jax.experimental.pallas import tpu as pltpu
from jax.sharding import PartitionSpec as P

MESH = pl.DeviceIdType.MESH
F32 = jnp.float32
BF16 = jnp.bfloat16
SPAN = 240.0
HALF = 120.0
LN2 = 0.6931471805599453
TINY = 1e-37
CHUNKS = 5
WITH_SUMS = 1
EXTRA = 3


def coords(shard):
    return shard // 8, (shard // 4) % 2, shard % 4


def ahead(me, off):
    z, y, x = coords(me)
    dz, dy, dx = coords(off)
    return ((z + dz) % 4) * 8 + ((y + dy) % 2) * 4 + (x + dx) % 4


def behind(me, off):
    z, y, x = coords(me)
    dz, dy, dx = coords(off)
    return ((z + 4 - dz) % 4) * 8 + ((y + 2 - dy) % 2) * 4 + (x + 4 - dx) % 4


def steps_to(off):
    dz, dy, dx = coords(off)
    return min(dz, 4 - dz) + dy + min(dx, 4 - dx)


def in_words(k):
    offs = sorted(off for off in range(32) if steps_to(off) == k)
    offs = sorted(offs, key=lambda off: off * 11 % 32)
    return [offs[i : i + 5] for i in range(0, len(offs), 5)]


STAGES = [in_words(k) for k in range(1, 6)]
STAGES[-1][-1].append(0)
NEAR = STAGES[0][0]


def each(word, body):
    def step(_, rest):
        body(rest % 32)
        return rest // 32

    lax.fori_loop(0, len(word), step, jnp.int32(sum(off * 32**i for i, off in enumerate(word))))


def turn(i, e):
    return (27 * (i + 1) + 9 * e) % 32


def to_all_lanes(tile, lane):
    return jnp.broadcast_to(tile[:, lane : lane + 1], tile.shape)


def exchange(train, other, weight, gain, ready, scale, router,
             tbuf, obuf, sbuf, rbuf, ssum, fbuf, part, pair, own_rows, rows_in, rows_out,
             first_t, first_o, load_t, load_o, stage_sem, send, send_more, recv, self_sem,
             pair_send, pair_recv, core_send, core_recv):
    experts, tiles = ready.shape[0], ready.shape[1]
    me = lax.axis_index("shard")
    group = lax.axis_index("expert")
    y_lo, core = group // 2, group % 2
    across = (1 - y_lo) * 2 + core
    beside = y_lo * 2 + (1 - core)

    barrier = pltpu.get_barrier_semaphore()
    for off in NEAR:
        pl.semaphore_signal(barrier, inc=1, device_id={"shard": ahead(me, off)}, device_id_type=MESH)
    for peer in (across, beside):
        pl.semaphore_signal(barrier, inc=1, device_id={"expert": peer}, device_id_type=MESH)

    words = [word for stage in STAGES for word in stage]
    for w, word in enumerate(words):
        def load_piece(off):
            at = pl.ds(ahead(me, off) * tiles, tiles)
            pltpu.make_async_copy(train.at[0, at], tbuf.at[0, at], first_t.at[w]).start()
            pltpu.make_async_copy(other.at[0, at], obuf.at[0, at], first_o.at[w]).start()

        each(word, load_piece)

    def wait_first(w):
        at = pl.ds(0, len(words[w]) * tiles)
        pltpu.make_async_copy(train.at[0, at], tbuf.at[0, at], first_t.at[w]).wait()
        pltpu.make_async_copy(other.at[0, at], obuf.at[0, at], first_o.at[w]).wait()

    loads = []
    for e in range(1, experts):
        of_expert = []
        for c in range(CHUNKS):
            part_of = pl.ds(c * (tiles * 32 // CHUNKS), tiles * 32 // CHUNKS)
            k = (e - 1) * CHUNKS + c
            of_expert += [
                pltpu.make_async_copy(train.at[e, part_of], tbuf.at[e, part_of], load_t.at[k]),
                pltpu.make_async_copy(other.at[e, part_of], obuf.at[e, part_of], load_o.at[k]),
            ]
        loads.append(of_expert)

    lanes = lax.broadcasted_iota(jnp.int32, (8, 128), 1)

    def latest(e, j, t):
        at = j * tiles + t
        return tbuf[e, at] + obuf[e, at].astype(F32)

    def sums_of(e):
        def body(k, _):
            for off in [k * 4 + step for step in range(4)]:
                j = ahead(me, off)
                tile = ssum[off]
                for t in range(tiles):
                    x = latest(e, j, t)
                    total = jnp.sum(x * x, axis=1, keepdims=True)
                    tile = jnp.where(lanes == e * tiles + t, total, tile)
                ssum[off] = tile
            return 0

        for copy in loads[e - 1]:
            copy.wait()
        lax.fori_loop(0, 8, body, 0)

    def tiles_of(e):
        return pl.ds(0, tiles + EXTRA if e == WITH_SUMS else tiles)

    def piece(e, off, peer):
        at = (e * 32 + off, tiles_of(e))
        return pltpu.make_async_remote_copy(
            sbuf.at[at], rbuf.at[at], send_more if e == WITH_SUMS else send, recv.at[e * 32 + off],
            device_id={"shard": peer}, device_id_type=MESH,
        )

    def send_piece(e, off):
        @pl.when(off != 0)
        def _():
            piece(e, off, ahead(me, off)).start()

    def code(x, inverse):
        share = jnp.maximum(jnp.abs(x) * inverse, 1e-30)
        level = jnp.exp2(share * lax.rsqrt(share) * SPAN - HALF)
        return jnp.where(x < 0, -level, level).astype(BF16)

    def encode_first(off):
        j = ahead(me, off)
        tile = jnp.zeros((8, 128), F32)
        for t in range(tiles):
            x = latest(0, j, t)
            total = jnp.sum(x * x, axis=1, keepdims=True)
            tile = jnp.where(lanes == t, total, tile)
            sbuf[off, t] = code(x, lax.rsqrt(jnp.maximum(total, TINY)))
        ssum[off] = tile

    def encode(e, off):
        j = ahead(me, off)
        inverse = lax.rsqrt(jnp.maximum(ssum[off], TINY))
        for t in range(tiles):
            sbuf[e * 32 + off, t] = code(latest(e, j, t), to_all_lanes(inverse, e * tiles + t))
        if e == WITH_SUMS:
            high = ssum[off].astype(BF16)
            sbuf[e * 32 + off, tiles] = high
            sbuf[e * 32 + off, tiles + 1] = (ssum[off] - high.astype(F32)).astype(BF16)
            sbuf[e * 32 + off, tiles + 2] = own_rows[...]

    def encode_all(e):
        def body(k, _):
            for step in range(2):
                encode(e, turn(2 * k + step, e))

            @pl.when(k > 0)
            def _():
                for step in range(2):
                    send_piece(e, turn(2 * k - 2 + step, e))

            return 0

        lax.fori_loop(0, 16, body, 0)
        for i in (30, 31):
            send_piece(e, turn(i, e))

    own = weight[...] * gain[...]
    part[...] = jnp.concatenate([own, jnp.zeros_like(own)], axis=0).astype(BF16)

    to_pair = pltpu.make_async_remote_copy(
        part, pair, pair_send, pair_recv, device_id={"expert": across}, device_id_type=MESH
    )
    w = 0
    for k, stage in enumerate(STAGES):
        for first, word in zip([True] + [False] * len(stage), stage):
            wait_first(w)
            w += 1
            for off in word:
                encode_first(off)
            if first:
                if k == 0:
                    pl.semaphore_wait(barrier, len(NEAR) + 2)
                else:
                    pl.semaphore_wait(stage_sem.at[k - 1], len(NEAR))
                if k < len(STAGES) - 1:
                    for off in NEAR:
                        pl.semaphore_signal(
                            stage_sem.at[k], inc=1, device_id={"shard": ahead(me, off)}, device_id_type=MESH
                        )
            for off in word:
                if off:
                    send_piece(0, off)
        if k == 0:
            to_pair.start()
            for of_expert in loads:
                for copy in of_expert:
                    copy.start()

    for e in range(1, experts):
        sums_of(e)

    to_pair.wait()
    mine, theirs = part[...].astype(F32)[:4], pair[...].astype(F32)[:4]
    low = jnp.where(y_lo == 0, mine, theirs)
    high = jnp.where(y_lo == 0, theirs, mine)
    own_rows[...] = jnp.concatenate([low, high], axis=0).astype(BF16)

    for e in range(1, experts):
        encode_all(e)
    keep = []
    for e in range(experts):
        at = (e * 32, tiles_of(e))
        keep.append(pltpu.make_async_copy(sbuf.at[at], rbuf.at[at], self_sem.at[e]))
        keep[e].start()

    def arrival(e, off):
        @pl.when(off != 0)
        def _():
            piece(e, off, behind(me, off)).wait_recv()

    def arrive(i, _):
        arrival(WITH_SUMS, turn(i, WITH_SUMS))
        return 0

    def sums_from(k):
        p = WITH_SUMS * 32 + k
        return rbuf[p, tiles].astype(F32) + rbuf[p, tiles + 1].astype(F32)

    keep[WITH_SUMS].wait()
    lax.fori_loop(0, 32, arrive, 0)
    total = lax.fori_loop(1, 32, lambda k, acc: acc + sums_from(k), sums_from(0))

    def factors(k, _):
        fbuf[k] = jnp.sqrt(sums_from(k) / total)
        rows_in[k] = rbuf[WITH_SUMS * 32 + k, tiles + 2]
        return 0

    lax.fori_loop(0, 32, factors, 0)
    norm = jnp.sqrt(total)
    wide = lax.broadcasted_iota(jnp.int32, (8, 256), 1) - lax.broadcasted_iota(jnp.int32, (8, 256), 0)
    for e in range(experts):
        spread = jnp.zeros((8, 256), F32)
        for t in range(tiles):
            column = norm[:, e * tiles + t : e * tiles + t + 1]
            spread = jnp.where(wide == t * 8, column, spread)
        scale[e : e + 1, :] = jnp.sum(spread, axis=0, keepdims=True)[:, : tiles * 8]

    def decode(e):
        def body(k, _):
            offs = [turn(2 * k + step, e) for step in range(2)]
            if e != WITH_SUMS:
                for off in offs:
                    arrival(e, off)
            for off in offs:
                factor = fbuf[off]
                source = behind(me, off)
                for t in range(tiles):
                    y = rbuf[e * 32 + off, t].astype(F32)
                    root = jnp.log(jnp.abs(y)) * (1.0 / (SPAN * LN2)) + HALF / SPAN
                    value = root * root * to_all_lanes(factor, e * tiles + t)
                    ready[e, t, source] = jnp.where(y < 0, -value, value).astype(BF16)
            return 0

        if e != WITH_SUMS:
            keep[e].wait()
        lax.fori_loop(0, 16, body, 0)

    decode(1)
    to_core = pltpu.make_async_remote_copy(
        rows_in, rows_out, core_send, core_recv, device_id={"expert": beside}, device_id_type=MESH
    )
    to_core.start()
    decode(0)
    to_core.wait()

    def place(k, _):
        a, b = rows_in[k].astype(F32), rows_out[k].astype(F32)
        first = jnp.where(core == 0, a, b)
        second = jnp.where(core == 0, b, a)
        block = jnp.concatenate([first[:4], second[:4], first[4:], second[4:]], axis=0)
        router[:, pl.ds(pl.multiple_of(behind(me, k) * 128, 128), 128)] = block.astype(BF16)
        return 0

    lax.fori_loop(0, 32, place, 0)
    for e in range(2, experts):
        decode(e)

    others = [e for e in range(experts) if e != WITH_SUMS]
    at = (pl.ds(0, 31 * len(others)), pl.ds(0, tiles))
    pltpu.make_async_remote_copy(
        sbuf.at[at], rbuf.at[at], send, recv.at[0], device_id={"shard": ahead(me, 1)}, device_id_type=MESH
    ).wait_send()
    at = (pl.ds(0, 31), tiles_of(WITH_SUMS))
    pltpu.make_async_remote_copy(
        sbuf.at[at], rbuf.at[at], send_more, recv.at[0], device_id={"shard": ahead(me, 1)}, device_id_type=MESH
    ).wait_send()


def deliver(ready_in, scale_in, router_in, ready, scale, router, sems):
    experts, tiles = ready.shape[:2]
    copies = [
        pltpu.make_async_copy(scale_in, scale, sems.at[experts * CHUNKS]),
        pltpu.make_async_copy(router_in, router, sems.at[experts * CHUNKS + 1]),
    ]
    for k in range(experts * CHUNKS):
        at = (k // CHUNKS, pl.ds(k % CHUNKS * (tiles // CHUNKS), tiles // CHUNKS))
        copies.append(pltpu.make_async_copy(ready_in.at[at], ready.at[at], sems.at[k]))
    for copy in copies:
        copy.start()
    for copy in copies:
        copy.wait()


def per_device(train_down, other_down, router_weight, router_gain):
    experts, inner, columns = train_down.shape
    tiles = inner // 32 // 8
    rows = inner // 8
    train = train_down.reshape(experts, rows, 8, columns)
    other = other_down.reshape(experts, rows, 8, columns)
    vmem = pl.BlockSpec(memory_space=pltpu.VMEM)
    anywhere = pl.BlockSpec(memory_space=pl.ANY)
    dma = pltpu.SemaphoreType.DMA
    pieces = experts * 32
    inside = pl.pallas_call(
        exchange,
        out_shape=(
            pltpu.VMEM((experts, tiles, 32, 8, columns), BF16),
            pltpu.VMEM((experts, tiles * 8), F32),
            pltpu.VMEM((16, 4096), BF16),
        ),
        in_specs=[anywhere, anywhere, vmem, vmem],
        out_specs=(vmem, vmem, vmem),
        scratch_shapes=[
            pltpu.VMEM((experts, rows, 8, columns), F32),
            pltpu.VMEM((experts, rows, 8, columns), BF16),
            pltpu.VMEM((pieces, tiles + EXTRA, 8, columns), BF16),
            pltpu.VMEM((pieces, tiles + EXTRA, 8, columns), BF16),
            pltpu.VMEM((32, 8, 128), F32),
            pltpu.VMEM((32, 8, 128), F32),
            pltpu.VMEM((8, 128), BF16),
            pltpu.VMEM((8, 128), BF16),
            pltpu.VMEM((8, 128), BF16),
            pltpu.VMEM((32, 8, 128), BF16),
            pltpu.VMEM((32, 8, 128), BF16),
            dma((sum(map(len, STAGES)),)), dma((sum(map(len, STAGES)),)),
            dma(((experts - 1) * CHUNKS,)), dma(((experts - 1) * CHUNKS,)),
            pltpu.SemaphoreType.REGULAR((len(STAGES) - 1,)), dma, dma, dma((pieces,)), dma((experts,)),
            dma, dma, dma, dma,
        ],
        compiler_params=pltpu.CompilerParams(
            collective_id=0, has_side_effects=True, vmem_limit_bytes=48 * 1024 * 1024
        ),
        name="exchange",
    )(train, other, router_weight.T, router_gain.reshape(1, -1))
    ready, scale, router = pl.pallas_call(
        deliver,
        out_shape=(
            jax.ShapeDtypeStruct((experts, tiles, 32, 8, columns), BF16),
            jax.ShapeDtypeStruct((experts, tiles * 8), F32),
            jax.ShapeDtypeStruct((16, 4096), BF16),
        ),
        in_specs=[vmem, vmem, vmem],
        out_specs=(anywhere, anywhere, anywhere),
        scratch_shapes=[dma((experts * CHUNKS + 2,))],
        compiler_params=pltpu.CompilerParams(vmem_limit_bytes=16 * 1024 * 1024),
        name="deliver",
    )(*inside)
    ready = ready.transpose(0, 1, 3, 2, 4).reshape(experts, tiles * 8, 32 * columns)
    return (ready, scale, router.T)


def solution(mesh):
    in_specs = (
        P("expert", None, "shard"),
        P("expert", None, "shard"),
        P("shard", "expert"),
        P("shard"),
    )
    out_specs = (P("expert", "shard", None), P("expert", "shard"), P())
    return jax.shard_map(
        per_device, mesh=mesh, in_specs=in_specs, out_specs=out_specs, check_vma=False
    )
```

time: 95.8 us -> 93.3 us (0.974)
  the two profiles are of different devices: /device:TPU:22 before, /device:TPU:18 now
where the time goes in v2:
time: 93.3 us; the launch traced here: 92.2 us
  Pallas kernels  91.6 us (98%)
    pallas_call x1, Pallas kernels, per_device(): pl.pallas_call(exchange, out_shape=(pltpu.VMEM((experts, tiles, 32, 8, co...  88.6 us
    pallas_call x1, Pallas kernels, per_device(): pl.pallas_call(deliver, out_shape=(jax.ShapeDtypeStruct((experts, tiles,...  2.96 us

profile of v2, /device:TPU:18, one launch (start us, length us, event | category | flops | bytes accessed | tf_op | source)
XLA Modules:
  0.0 92.2 jit_solution(13807810505561292605)
XLA Ops:
  0.6 88.6 %exchange.1 = (bf16[4,25,32,8,128]{4,3,2,1,0:T(8,128)(2,1)S(1)}, f32[4,200]{1,0:T(4,128)S(1)}, bf16[16,4096]{1,0:T(8,128)(2,1)S(1)}) custom-call(f32[4,800,8,128]{3,2,1,0:T(8,128)} %bitcast.8, bf16[4,800,8,128]{3,2,1,0:T(8,128)(2,1)} %bitcast.9, f32[4,128]{1,0:T(4,128)} %bitcast.10, f32[1,128]{1,0:T(1,128)} %bitcast.11), custom_call_target="tpu_custom_call" | custom-call | tf_op jit(solution)/shard_map/exchange/pallas_call | solution.py:349
  89.3 3.0 %deliver.1 = (bf16[4,25,32,8,128]{4,3,2,1,0:T(8,128)(2,1)}, f32[4,200]{1,0:T(4,128)}, bf16[16,4096]{1,0:T(8,128)(2,1)}) custom-call(bf16[4,25,32,8,128]{4,3,2,1,0:T(8,128)(2,1)S(1)} %get-tuple-element.9.ready_in, f32[4,200]{1,0:T(4,128)S(1)} %get-tuple-element.10.scale_in, bf16[16,4096]{1,0:T(8,128)(2,1)S(1)} %get-tuple-element.11.router_in), custom_call_target="tpu_custom_call" | custom-call | tf_op jit(solution)/shard_map/deliver/pallas_call | solution.py:380

commit v3 on v2

--- a/solution.py
+++ b/solution.py
@@ -15,8 +15,11 @@
 LN2 = 0.6931471805599453
 TINY = 1e-37
 CHUNKS = 5
-WITH_SUMS = 1
-EXTRA = 3
+ALONE = 2
+WITH_ROWS = 2
+EXTRA = 1
+STRIDE = (27, 27, 27, 27)
+SHIFT = (0, 14, 14, 29)
 
 
 def coords(shard):
@@ -60,17 +63,17 @@
 
 
 def turn(i, e):
-    return (27 * (i + 1) + 9 * e) % 32
+    return (STRIDE[e] * (i + 1) + SHIFT[e]) % 32
 
 
 def to_all_lanes(tile, lane):
     return jnp.broadcast_to(tile[:, lane : lane + 1], tile.shape)
 
 
-def exchange(train, other, weight, gain, ready, scale, router,
-             tbuf, obuf, sbuf, rbuf, ssum, fbuf, part, pair, own_rows, rows_in, rows_out,
+def exchange(train, other, weight_in, gain_in, ready, scale, router,
+             weight, gain, small_sem, tbuf, obuf, sbuf, rbuf, ssum, rsum, fbuf, part, pair, own_rows, rows_in, rows_out,
              first_t, first_o, load_t, load_o, stage_sem, send, send_more, recv, self_sem,
-             pair_send, pair_recv, core_send, core_recv):
+             sum_send, sum_recv, pair_send, pair_recv, core_send, core_recv):
     experts, tiles = ready.shape[0], ready.shape[1]
     me = lax.axis_index("shard")
     group = lax.axis_index("expert")
@@ -133,12 +136,12 @@
         lax.fori_loop(0, 8, body, 0)
 
     def tiles_of(e):
-        return pl.ds(0, tiles + EXTRA if e == WITH_SUMS else tiles)
+        return pl.ds(0, tiles + EXTRA if e == WITH_ROWS else tiles)
 
     def piece(e, off, peer):
         at = (e * 32 + off, tiles_of(e))
         return pltpu.make_async_remote_copy(
-            sbuf.at[at], rbuf.at[at], send_more if e == WITH_SUMS else send, recv.at[e * 32 + off],
+            sbuf.at[at], rbuf.at[at], send_more if e == WITH_ROWS else send, recv.at[e * 32 + off],
             device_id={"shard": peer}, device_id_type=MESH,
         )
 
@@ -152,14 +155,14 @@
         level = jnp.exp2(share * lax.rsqrt(share) * SPAN - HALF)
         return jnp.where(x < 0, -level, level).astype(BF16)
 
-    def encode_first(off):
+    def encode_first(e, off):
         j = ahead(me, off)
-        tile = jnp.zeros((8, 128), F32)
+        tile = jnp.zeros((8, 128), F32) if e == 0 else ssum[off]
         for t in range(tiles):
-            x = latest(0, j, t)
+            x = latest(e, j, t)
             total = jnp.sum(x * x, axis=1, keepdims=True)
-            tile = jnp.where(lanes == t, total, tile)
-            sbuf[off, t] = code(x, lax.rsqrt(jnp.maximum(total, TINY)))
+            tile = jnp.where(lanes == e * tiles + t, total, tile)
+            sbuf[e * 32 + off, t] = code(x, lax.rsqrt(jnp.maximum(total, TINY)))
         ssum[off] = tile
 
     def encode(e, off):
@@ -167,16 +170,13 @@
         inverse = lax.rsqrt(jnp.maximum(ssum[off], TINY))
         for t in range(tiles):
             sbuf[e * 32 + off, t] = code(latest(e, j, t), to_all_lanes(inverse, e * tiles + t))
-        if e == WITH_SUMS:
-            high = ssum[off].astype(BF16)
-            sbuf[e * 32 + off, tiles] = high
-            sbuf[e * 32 + off, tiles + 1] = (ssum[off] - high.astype(F32)).astype(BF16)
-            sbuf[e * 32 + off, tiles + 2] = own_rows[...]
+        if e == WITH_ROWS:
+            sbuf[e * 32 + off, tiles] = own_rows[...]
 
     def encode_all(e):
         def body(k, _):
             for step in range(2):
-                encode(e, turn(2 * k + step, e))
+                (encode if e >= ALONE else encode_first)(e, turn(2 * k + step, e))
 
             @pl.when(k > 0)
             def _():
@@ -189,8 +189,12 @@
         for i in (30, 31):
             send_piece(e, turn(i, e))
 
-    own = weight[...] * gain[...]
-    part[...] = jnp.concatenate([own, jnp.zeros_like(own)], axis=0).astype(BF16)
+    small = [
+        pltpu.make_async_copy(weight_in, weight, small_sem.at[0]),
+        pltpu.make_async_copy(gain_in, gain, small_sem.at[1]),
+    ]
+    for copy in small:
+        copy.start()
 
     to_pair = pltpu.make_async_remote_copy(
         part, pair, pair_send, pair_recv, device_id={"expert": across}, device_id_type=MESH
@@ -201,7 +205,7 @@
             wait_first(w)
             w += 1
             for off in word:
-                encode_first(off)
+                encode_first(0, off)
             if first:
                 if k == 0:
                     pl.semaphore_wait(barrier, len(NEAR) + 2)
@@ -216,12 +220,19 @@
                 if off:
                     send_piece(0, off)
         if k == 0:
-            to_pair.start()
+            for copy in small:
+                copy.wait()
+            own = weight[...] * gain[...]
+            part[...] = jnp.concatenate([own, jnp.zeros_like(own)], axis=0).astype(BF16)
             for of_expert in loads:
                 for copy in of_expert:
                     copy.start()
 
-    for e in range(1, experts):
+    to_pair.start()
+    for copy in loads[0]:
+        copy.wait()
+    encode_all(1)
+    for e in range(ALONE, experts):
         sums_of(e)
 
     to_pair.wait()
@@ -230,7 +241,22 @@
     high = jnp.where(y_lo == 0, theirs, mine)
     own_rows[...] = jnp.concatenate([low, high], axis=0).astype(BF16)
 
-    for e in range(1, experts):
+    rsum[0] = ssum[0]
+
+    def send_sums(i, _):
+        off = turn(i, 0)
+
+        @pl.when(off != 0)
+        def _():
+            pltpu.make_async_remote_copy(
+                ssum.at[off], rsum.at[off], sum_send, sum_recv,
+                device_id={"shard": ahead(me, off)}, device_id_type=MESH,
+            ).start()
+
+        return 0
+
+    lax.fori_loop(0, 32, send_sums, 0)
+    for e in range(ALONE, experts):
         encode_all(e)
     keep = []
     for e in range(experts):
@@ -243,21 +269,15 @@
         def _():
             piece(e, off, behind(me, off)).wait_recv()
 
-    def arrive(i, _):
-        arrival(WITH_SUMS, turn(i, WITH_SUMS))
-        return 0
-
-    def sums_from(k):
-        p = WITH_SUMS * 32 + k
-        return rbuf[p, tiles].astype(F32) + rbuf[p, tiles + 1].astype(F32)
-
-    keep[WITH_SUMS].wait()
-    lax.fori_loop(0, 32, arrive, 0)
-    total = lax.fori_loop(1, 32, lambda k, acc: acc + sums_from(k), sums_from(0))
+    all_sums = pltpu.make_async_remote_copy(
+        ssum.at[pl.ds(1, 31)], rsum.at[pl.ds(1, 31)], sum_send, sum_recv,
+        device_id={"shard": ahead(me, 1)}, device_id_type=MESH,
+    )
+    all_sums.wait_recv()
+    total = lax.fori_loop(1, 32, lambda k, acc: acc + rsum[k], rsum[0])
 
     def factors(k, _):
-        fbuf[k] = jnp.sqrt(sums_from(k) / total)
-        rows_in[k] = rbuf[WITH_SUMS * 32 + k, tiles + 2]
+        fbuf[k] = jnp.sqrt(rsum[k] / total)
         return 0
 
     lax.fori_loop(0, 32, factors, 0)
@@ -270,12 +290,11 @@
             spread = jnp.where(wide == t * 8, column, spread)
         scale[e : e + 1, :] = jnp.sum(spread, axis=0, keepdims=True)[:, : tiles * 8]
 
-    def decode(e):
+    def decode(e, after_first=None):
         def body(k, _):
             offs = [turn(2 * k + step, e) for step in range(2)]
-            if e != WITH_SUMS:
-                for off in offs:
-                    arrival(e, off)
+            for off in offs:
+                arrival(e, off)
             for off in offs:
                 factor = fbuf[off]
                 source = behind(me, off)
@@ -286,16 +305,27 @@
                     ready[e, t, source] = jnp.where(y < 0, -value, value).astype(BF16)
             return 0
 
-        if e != WITH_SUMS:
-            keep[e].wait()
-        lax.fori_loop(0, 16, body, 0)
-
-    decode(1)
+        keep[e].wait()
+        if after_first is None:
+            lax.fori_loop(0, 16, body, 0)
+        else:
+            body(0, 0)
+            after_first()
+            lax.fori_loop(1, 16, body, 0)
+
+    for e in range(WITH_ROWS + 1):
+        decode(e)
+
+    def take_rows(k, _):
+        rows_in[k] = rbuf[WITH_ROWS * 32 + k, tiles]
+        return 0
+
+    lax.fori_loop(0, 32, take_rows, 0)
     to_core = pltpu.make_async_remote_copy(
         rows_in, rows_out, core_send, core_recv, device_id={"expert": beside}, device_id_type=MESH
     )
-    to_core.start()
-    decode(0)
+    for e in range(WITH_ROWS + 1, experts):
+        decode(e, to_core.start)
     to_core.wait()
 
     def place(k, _):
@@ -307,15 +337,14 @@
         return 0
 
     lax.fori_loop(0, 32, place, 0)
-    for e in range(2, experts):
-        decode(e)
-
-    others = [e for e in range(experts) if e != WITH_SUMS]
+    all_sums.wait_send()
+
+    others = [e for e in range(experts) if e != WITH_ROWS]
     at = (pl.ds(0, 31 * len(others)), pl.ds(0, tiles))
     pltpu.make_async_remote_copy(
         sbuf.at[at], rbuf.at[at], send, recv.at[0], device_id={"shard": ahead(me, 1)}, device_id_type=MESH
     ).wait_send()
-    at = (pl.ds(0, 31), tiles_of(WITH_SUMS))
+    at = (pl.ds(0, 31), tiles_of(WITH_ROWS))
     pltpu.make_async_remote_copy(
         sbuf.at[at], rbuf.at[at], send_more, recv.at[0], device_id={"shard": ahead(me, 1)}, device_id_type=MESH
     ).wait_send()
@@ -353,13 +382,17 @@
             pltpu.VMEM((experts, tiles * 8), F32),
             pltpu.VMEM((16, 4096), BF16),
         ),
-        in_specs=[anywhere, anywhere, vmem, vmem],
+        in_specs=[anywhere, anywhere, anywhere, anywhere],
         out_specs=(vmem, vmem, vmem),
         scratch_shapes=[
+            pltpu.VMEM((experts, columns), F32),
+            pltpu.VMEM((1, columns), F32),
+            dma((2,)),
             pltpu.VMEM((experts, rows, 8, columns), F32),
             pltpu.VMEM((experts, rows, 8, columns), BF16),
             pltpu.VMEM((pieces, tiles + EXTRA, 8, columns), BF16),
             pltpu.VMEM((pieces, tiles + EXTRA, 8, columns), BF16),
+            pltpu.VMEM((32, 8, 128), F32),
             pltpu.VMEM((32, 8, 128), F32),
             pltpu.VMEM((32, 8, 128), F32),
             pltpu.VMEM((8, 128), BF16),
@@ -370,7 +403,7 @@
             dma((sum(map(len, STAGES)),)), dma((sum(map(len, STAGES)),)),
             dma(((experts - 1) * CHUNKS,)), dma(((experts - 1) * CHUNKS,)),
             pltpu.SemaphoreType.REGULAR((len(STAGES) - 1,)), dma, dma, dma((pieces,)), dma((experts,)),
-            dma, dma, dma, dma,
+            dma, dma, dma, dma, dma, dma,
         ],
         compiler_params=pltpu.CompilerParams(
             collective_id=0, has_side_effects=True, vmem_limit_bytes=48 * 1024 * 1024

time: 93.3 us -> 91 us (0.975)
  Pallas kernels: 91.6 us -> 89.3 us
    pallas_call x1, Pallas kernels: 88.6 us -> 86.4 us  [per_device(): pl.pallas_call(exchange, out_shape=(pltpu.VMEM((experts, tiles, 32, 8, co...]
where the time goes in v3:
time: 91 us; the launch traced here: 89.9 us
  Pallas kernels  89.3 us (98%)
    pallas_call x1, Pallas kernels, per_device(): pl.pallas_call(exchange, out_shape=(pltpu.VMEM((experts, tiles, 32, 8, co...  86.4 us
    pallas_call x1, Pallas kernels, per_device(): pl.pallas_call(deliver, out_shape=(jax.ShapeDtypeStruct((experts, tiles,...  2.96 us

profile of v3, /device:TPU:18, one launch (start us, length us, event | category | flops | bytes accessed | tf_op | source)
XLA Modules:
  0.0 89.9 jit_solution(12244937155094153847)
XLA Ops:
  0.6 86.4 %exchange.1 = (bf16[4,25,32,8,128]{4,3,2,1,0:T(8,128)(2,1)S(1)}, f32[4,200]{1,0:T(4,128)S(1)}, bf16[16,4096]{1,0:T(8,128)(2,1)S(1)}) custom-call(f32[4,800,8,128]{3,2,1,0:T(8,128)} %bitcast.8, bf16[4,800,8,128]{3,2,1,0:T(8,128)(2,1)} %bitcast.9, f32[4,128]{1,0:T(4,128)} %bitcast.10, f32[1,128]{1,0:T(1,128)} %bitcast.11), custom_call_target="tpu_custom_call" | custom-call | tf_op jit(solution)/shard_map/exchange/pallas_call | solution.py:378
  87.0 3.0 %deliver.1 = (bf16[4,25,32,8,128]{4,3,2,1,0:T(8,128)(2,1)}, f32[4,200]{1,0:T(4,128)}, bf16[16,4096]{1,0:T(8,128)(2,1)}) custom-call(bf16[4,25,32,8,128]{4,3,2,1,0:T(8,128)(2,1)S(1)} %get-tuple-element.9.ready_in, f32[4,200]{1,0:T(4,128)S(1)} %get-tuple-element.10.scale_in, bf16[16,4096]{1,0:T(8,128)(2,1)S(1)} %get-tuple-element.11.router_in), custom_call_target="tpu_custom_call" | custom-call | tf_op jit(solution)/shard_map/deliver/pallas_call | solution.py:413

commit v4 on v3

--- a/solution.py
+++ b/solution.py
@@ -19,7 +19,7 @@
 WITH_ROWS = 2
 EXTRA = 1
 STRIDE = (27, 27, 27, 27)
-SHIFT = (0, 14, 14, 29)
+SHIFT = (0, 10, 7, 20)
 
 
 def coords(shard):
@@ -351,14 +351,12 @@
 
 
 def deliver(ready_in, scale_in, router_in, ready, scale, router, sems):
-    experts, tiles = ready.shape[:2]
-    copies = [
-        pltpu.make_async_copy(scale_in, scale, sems.at[experts * CHUNKS]),
-        pltpu.make_async_copy(router_in, router, sems.at[experts * CHUNKS + 1]),
+    experts = ready.shape[0]
+    copies = [pltpu.make_async_copy(ready_in.at[e], ready.at[e], sems.at[e]) for e in range(experts)]
+    copies += [
+        pltpu.make_async_copy(scale_in, scale, sems.at[experts]),
+        pltpu.make_async_copy(router_in, router, sems.at[experts + 1]),
     ]
-    for k in range(experts * CHUNKS):
-        at = (k // CHUNKS, pl.ds(k % CHUNKS * (tiles // CHUNKS), tiles // CHUNKS))
-        copies.append(pltpu.make_async_copy(ready_in.at[at], ready.at[at], sems.at[k]))
     for copy in copies:
         copy.start()
     for copy in copies:
@@ -419,7 +417,7 @@
         ),
         in_specs=[vmem, vmem, vmem],
         out_specs=(anywhere, anywhere, anywhere),
-        scratch_shapes=[dma((experts * CHUNKS + 2,))],
+        scratch_shapes=[dma((experts + 2,))],
         compiler_params=pltpu.CompilerParams(vmem_limit_bytes=16 * 1024 * 1024),
         name="deliver",
     )(*inside)

time: 91 us -> 89.9 us (0.988)
  Pallas kernels: 89.3 us -> 87.8 us
    pallas_call x1, Pallas kernels: 86.4 us -> 84.9 us  [per_device(): pl.pallas_call(exchange, out_shape=(pltpu.VMEM((experts, tiles, 32, 8, co...]
where the time goes in v4:
time: 89.9 us; the launch traced here: 88.4 us
  Pallas kernels  87.8 us (98%)
    pallas_call x1, Pallas kernels, per_device(): pl.pallas_call(exchange, out_shape=(pltpu.VMEM((experts, tiles, 32, 8, co...  84.9 us
    pallas_call x1, Pallas kernels, per_device(): pl.pallas_call(deliver, out_shape=(jax.ShapeDtypeStruct((experts, tiles,...  2.84 us

profile of v4, /device:TPU:18, one launch (start us, length us, event | category | flops | bytes accessed | tf_op | source)
XLA Modules:
  0.0 88.4 jit_solution(10427914678648259659)
XLA Ops:
  0.6 84.9 %exchange.1 = (bf16[4,25,32,8,128]{4,3,2,1,0:T(8,128)(2,1)S(1)}, f32[4,200]{1,0:T(4,128)S(1)}, bf16[16,4096]{1,0:T(8,128)(2,1)S(1)}) custom-call(f32[4,800,8,128]{3,2,1,0:T(8,128)} %bitcast.8, bf16[4,800,8,128]{3,2,1,0:T(8,128)(2,1)} %bitcast.9, f32[4,128]{1,0:T(4,128)} %bitcast.10, f32[1,128]{1,0:T(1,128)} %bitcast.11), custom_call_target="tpu_custom_call" | custom-call | tf_op jit(solution)/shard_map/exchange/pallas_call | solution.py:376
  85.6 2.8 %deliver.1 = (bf16[4,25,32,8,128]{4,3,2,1,0:T(8,128)(2,1)}, f32[4,200]{1,0:T(4,128)}, bf16[16,4096]{1,0:T(8,128)(2,1)}) custom-call(bf16[4,25,32,8,128]{4,3,2,1,0:T(8,128)(2,1)S(1)} %get-tuple-element.9.ready_in, f32[4,200]{1,0:T(4,128)S(1)} %get-tuple-element.10.scale_in, bf16[16,4096]{1,0:T(8,128)(2,1)S(1)} %get-tuple-element.11.router_in), custom_call_target="tpu_custom_call" | custom-call | tf_op jit(solution)/shard_map/deliver/pallas_call | solution.py:411
